TPU v7x, 128 devices: a whole 4x4x4 slice. The times are simulated.
128 devices in a mesh: dp: 8 (over z, core), mp: 16 (over y, x).
Axes of the slice: x: 4, y: 4, z: 4, core: 2. Of those that a mesh axis runs over, the one named last changes fastest.
Arguments:
- crop_hidden: bfloat16 [8, 1536, 8192], P(None, 'dp', 'mp'), may hold values from -15 to 15
- projector_weight: bfloat16 [8192, 8192], P('mp'), may hold values from -0.21213203 to 0.21213203
- pairing: int32 [8, 1536], P(None, 'dp'), may hold values from 0 to 191, as said below
Outputs:
- embeddings: float32 [8192, 8, 1536], P('mp', 'dp')
- loss_terms: float32 [4], replicated
Inputs may be any that keep to these rules, and one draw needn't show every extreme that they name: Each aligned block of 192 entries of a row of pairing is a permutation of 0 to 191.
All inputs are finite; a program needn't handle non-finite values.
Results may differ from a plain program's by a relative error of at most 0.0003.
Values may be sent and summed in bfloat16 or wider, within the bound.
No kernel may reach another device: no remote copies, remote signals or barrier semaphores. Data moves between devices by JAX's collectives and lax.ppermute only.
A program may use at most 128 MiB of HBM per device.

v0:
```python
import functools
import jax
import jax.numpy as jnp
from jax import lax
from jax.sharding import Mesh
from jax.sharding import PartitionSpec as P

MP = ("mp_0", "mp_1")
DP = ("dp_0", "dp_1")
DP_MP = ("dp_0", "dp_1", "mp_0", "mp_1")
highest = lax.Precision.HIGHEST
epsilon = 0.0001


def by_axis(x, axes):
    return functools.reduce(lax.psum, axes, x)


def local(crop_hidden, projector_weight, pairing):
    crop_count, local_rows, width_part = crop_hidden.shape
    features = projector_weight.shape[1]
    total_rows = crop_count * local_rows
    column_block = lax.all_to_all(projector_weight, MP, split_axis=1, concat_axis=0, tiled=True)
    shards = lax.all_gather(crop_hidden, MP, axis=2, tiled=True)
    flat_piece = shards.reshape(total_rows, shards.shape[2])
    embedded = lax.dot_general(
        column_block, flat_piece, (((0,), (1,)), ((), ())), preferred_element_type=jnp.float32
    )
    feature_part = embedded.shape[0]
    by_crop = embedded.reshape(feature_part, crop_count, local_rows)
    onehot = (pairing[:, :, None] == jnp.arange(local_rows, dtype=jnp.int32)[None, None, :]).astype(
        jnp.float32
    )
    aligned = jnp.einsum("jcr,cri->jci", by_crop, onehot, precision=highest)
    invariance = 0.0
    for anchor in range(2):
        differ = aligned - aligned[:, anchor : anchor + 1, :]
        invariance = invariance + jnp.sum(differ * differ)
    owned_block = lax.all_to_all(by_crop, DP, split_axis=1, concat_axis=2, tiled=True)
    batch_rows = owned_block.shape[2]
    column_mean = jnp.mean(owned_block, axis=2, keepdims=True)
    centered = owned_block - column_mean
    variance = jnp.sum(centered * centered, axis=2) / (batch_rows - 1)
    hinge_sum = jnp.sum(jax.nn.relu(1.0 - jnp.sqrt(variance + epsilon)))
    diagonal_sq = jnp.sum(variance * variance)
    gram_scale = 1.0 / ((batch_rows - 1) * (batch_rows - 1))
    partial_gram = jnp.einsum("jcr,jcs->crs", centered, centered, precision=highest)
    gram_block = lax.psum(partial_gram.astype(jnp.bfloat16), MP).astype(jnp.float32)
    frobenius = jnp.where(
        lax.axis_index(MP) == 0, jnp.sum(gram_block * gram_block) * gram_scale, 0.0
    )
    totals = (
        by_axis(invariance, DP_MP),
        by_axis(hinge_sum, DP_MP),
        by_axis(frobenius - diagonal_sq, DP_MP),
    )
    invariance_loss = totals[0] / (2 * (crop_count - 1) * batch_rows * features)
    variance_loss = totals[1] / (crop_count * features)
    covariance_loss = totals[2] / (crop_count * features)
    total_loss = 25.0 * invariance_loss + 25.0 * variance_loss + covariance_loss
    loss_terms = jnp.stack([invariance_loss, variance_loss, covariance_loss, total_loss])
    return (owned_block, loss_terms)


def solution(mesh):
    torus = Mesh(mesh.devices.reshape(4, 2, 4, 4), ("dp_0", "dp_1", "mp_0", "mp_1"))
    placed = (P(None, DP, MP), P(MP, None), P(None, DP))
    return jax.shard_map(
        local, mesh=torus, in_specs=placed, out_specs=(P(MP, DP, None), P()), check_vma=False
    )
```

profile of v0, /device:TPU:0, one launch (start us, length us, event | category | flops | bytes accessed | tf_op | source)
XLA Modules:
  0.0 498.9 jit_solution(17605152332946094416)
XLA Ops:
  7.2 0.0 all-gather.2.cloned.1.call-start
  7.2 0.7 all-gather.2.cloned.1.call-update
  7.9 0.0 all-reduce.6.cloned.1.call-start
  7.9 7.5 %copy.9 = bf16[64,16,8,512]{3,2,0,1:T(8,128)(2,1)} copy(bf16[64,16,8,512]{3,2,1,0:T(8,128)(2,1)} %bitcast.30) | data formatting | bytes 16777216 | tf_op jit(solution)/shard_map/all_to_all | solution.py:23
  15.4 128.3 %all_to_all.31 = bf16[512,16,512]{2,0,1:T(8,128)(2,1)} all-to-all(bf16[512,16,512]{2,0,1:T(8,128)(2,1)} %bitcast.29), channel_id=1, replica_groups=mesh['dp_0'=4,'dp_1'=2,'mp_0'=4,'mp_1'=4] {'mp_0','mp_1'}, dimensions={1} | all-to-all | bytes 16777216 | tf_op jit(solution)/shard_map/all_to_all | solution.py:23
  143.8 117.0 %all-gather.2.cloned.1.call-done = bf16[8,192,8192]{2,1,0:T(8,128)(2,1)} async-done(((bf16[8,192,512]{2,1,0:T(8,128)(2,1)}), bf16[8,192,8192]{2,1,0:T(8,128)(2,1)}) %all-gather.2.cloned.1.call-update) | async-done | bytes 25165840 | tf_op jit(solution)/shard_map/all_gather | solution.py:24
  260.8 18.9 %fusion.2 = f32[512,8,192]{0,2,1:T(8,128)S(1)} fusion(bf16[8192,512,1]{1,0,2:T(8,128)(2,1)} %bitcast.31, bf16[8,192,8192]{2,1,0:T(8,128)(2,1)} %all-gather.2.cloned.1.call-done), kind=kOutput, calls=%fused_computation.17 | convolution fusion | flops 12884901888 | bytes 36700160 | tf_op jit(solution)/shard_map/dot_general | solution.py:26
  279.7 0.0 copy-start
  279.7 1.7 copy-done
  281.3 42.7 %all_to_all.32 = f32[512,8,192]{0,2,1:T(8,128)S(1)} all-to-all(f32[512,8,192]{0,2,1:T(8,128)S(1)} %fusion.2), channel_id=1, replica_groups=mesh['dp_0'=4,'dp_1'=2,'mp_0'=4,'mp_1'=4] {'dp_0','dp_1'}, dimensions={1} | all-to-all | bytes 6291456 | tf_op jit(solution)/shard_map/all_to_all | solution.py:39
  324.0 0.3 reduce_sum.65
  324.3 0.6 multiply_reduce_fusion.1
  324.8 16.8 %fusion = bf16[1,1536,1536]{2,1,0:T(8,128)(2,1)} fusion(f32[512,1536]{0,1:T(8,128)S(1)} %bitcast.32), kind=kOutput, calls=%fused_computation.3 | convolution fusion | flops 14497873920 | bytes 7864320 | tf_op jit(solution)/shard_map/jcr,jcs->crs/dot_general | solution.py:47
  341.6 0.0 copy-start.1
  341.6 0.0 all-reduce.6.cloned.1.call-update
  341.6 0.7 copy-done.1
  342.3 3.9 convolution_bitcast_fusion
  346.2 0.1 slice_bitcast_fusion.1
  346.2 2.0 multiply_reduce_fusion.2
  349.5 5.4 %copy.6 = f32[512,1,1536]{2,1,0:T(1,128)} copy(f32[512,1,1536]{0,2,1:T(8,128)S(1)} %bitcast.28) | data formatting | bytes 6291456
  354.9 0.7 multiply_reduce_fusion.4
  355.6 91.4 %all-reduce.6.cloned.1.call-done = bf16[1,1536,1536]{2,1,0:T(8,128)(2,1)} async-done(((bf16[1,1536,1536]{2,1,0:T(8,128)(2,1)}), bf16[1,1536,1536]{2,1,0:T(8,128)(2,1)}) %all-reduce.6.cloned.1.call-update) | async-done | bytes 4718608 | tf_op jit(solution)/shard_map/psum | solution.py:48
  447.0 5.3 %multiply_reduce_fusion = f32[]{:T(128)} fusion(bf16[1,1536,1536]{2,1,0:T(8,128)(2,1)} %all-reduce.6.cloned.1.call-done), kind=kLoop, calls=%fused_computation | loop fusion | flops 7077887 | bytes 4718596 | tf_op jit(solution)/shard_map/reduce_sum | solution.py:50
  453.5 11.3 %all-reduce.2 = (f32[]{:T(128)}, f32[]{:T(128)}, f32[]{:T(128)}) all-reduce(f32[]{:T(128)S(6)} %add.47, f32[]{:T(128)} %get-tuple-element.7, f32[]{:T(128)S(6)} %sub.61), channel_id=1, replica_groups=mesh['dp_0'=4,'dp_1'=2,'mp_0'=4,'mp_1'=4] {'dp_0'}, use_global_device_ids=true, to_apply=%region_2.0 | all-reduce | flops 3 | bytes 24 | tf_op jit(solution)/shard_map/psum | solution.py:16
  464.8 3.2 all-reduce.3
  467.9 11.0 %all-reduce.1 = (f32[]{:T(128)}, f32[]{:T(128)}, f32[]{:T(128)}) all-reduce(f32[]{:T(128)} %get-tuple-element.17, f32[]{:T(128)} %get-tuple-element.18, f32[]{:T(128)} %get-tuple-element.19), channel_id=1, replica_groups=mesh['dp_0'=4,'dp_1'=2,'mp_0'=4,'mp_1'=4] {'mp_0'}, use_global_device_ids=true, to_apply=%region_4.5 | all-reduce | flops 3 | bytes 24 | tf_op jit(solution)/shard_map/psum | solution.py:16
  478.9 9.4 %all-reduce = (f32[]{:T(128)}, f32[]{:T(128)}, f32[]{:T(128)}) all-reduce(f32[]{:T(128)} %get-tuple-element.11, f32[]{:T(128)} %get-tuple-element.12, f32[]{:T(128)} %get-tuple-element.13), channel_id=1, replica_groups=mesh['dp_0'=4,'dp_1'=2,'mp_0'=4,'mp_1'=4] {'mp_1'}, use_global_device_ids=true, to_apply=%region_5.6 | all-reduce | flops 3 | bytes 24 | tf_op jit(solution)/shard_map/psum | solution.py:16
  491.5 0.6 pad_maximum_fusion
  (1 shorter events, 0.0 us)
Async XLA Ops:
  7.2 253.6 %all-gather.2.cloned.1.call-start = ((), (), s32[]{:S(2)}) async-start(), calls=%async_computation.2 | async-start | bytes 26738688 | tf_op jit(solution)/shard_map/all_gather | solution.py:24
  7.9 439.1 %all-reduce.6.cloned.1.call-start = ((), (), s32[]{:S(2)}) async-start(), calls=%async_computation.3 | async-start | bytes 9437184 | tf_op jit(solution)/shard_map/psum | solution.py:48
  279.7 1.7 copy-start
  341.6 0.7 copy-start.1
Sparse Core Ops, SparseCore 0:
  10.1 250.6 all-gather.1
  341.7 105.2 all-reduce.5
where the time goes:
time: 499 us
  waiting for transfers between devices  209 us (42%)
  blocking collectives  206 us (41%)
  matrix products  39.5 us (8%)
  between operations  19.8 us (4%)
  local copies, waits for them, and re-layouts  15.3 us (3%)
  other arithmetic  9.4 us (2%)
    all_to_all x1, blocking collectives, local(): lax.all_to_all(projector_weight, MP, split_axis=1, concat_axis=0, tiled=T...  128 us
    all_gather x1, waiting for transfers between devices, local(): shards = lax.all_gather(crop_hidden, MP, axis=2, tiled=True)  117 us
    psum x1, waiting for transfers between devices, local(): lax.psum(partial_gram.astype(jnp.bfloat16), MP).astype(jnp.float32)  91.4 us
    all_to_all x1, blocking collectives, local(): lax.all_to_all(by_crop, DP, split_axis=1, concat_axis=2, tiled=True)  42.7 us
    psum x4, blocking collectives, by_axis(): return functools.reduce(lax.psum, axes, x)  34.8 us
    dot_general x1, matrix products, local(): lax.dot_general(column_block, flat_piece, (((0,), (1,)), ((), ())), prefe...  18.9 us
    dot_general x1, matrix products, local(): jnp.einsum('jcr,jcs->crs', centered, centered, precision=highest)  16.8 us
  transfers between devices with their start and end apart: 2, of which 2 were waited for; matrix products, arithmetic and copies ran while one was open for 4% of the time, Pallas kernels for 0%

commit v1 on v0

--- a/solution.py
+++ b/solution.py
@@ -21,7 +21,9 @@
     features = projector_weight.shape[1]
     total_rows = crop_count * local_rows
     column_block = lax.all_to_all(projector_weight, MP, split_axis=1, concat_axis=0, tiled=True)
-    shards = lax.all_gather(crop_hidden, MP, axis=2, tiled=True)
+    shards = jnp.concatenate(
+        lax.all_to_all(jnp.stack([crop_hidden] * lax.axis_size(MP)), MP, 0, 0), axis=2
+    )
     flat_piece = shards.reshape(total_rows, shards.shape[2])
     embedded = lax.dot_general(
         column_block, flat_piece, (((0,), (1,)), ((), ())), preferred_element_type=jnp.float32

time: 499 us -> 656 us (1.31)
  blocking collectives: 206 us -> 462 us
  waiting for transfers between devices: 209 us -> 89.2 us
  local copies, waits for them, and re-layouts: 15.3 us -> 34.9 us
    all_to_all x0 -> x1, blocking collectives: none -> 281 us  [local(): lax.all_to_all(jnp.stack([crop_hidden] * lax.axis_size(MP)), MP, 0, 0)]
    all_gather x1 -> x0, waiting for transfers between devices: 117 us -> none  [local(): shards = lax.all_gather(crop_hidden, MP, axis=2, tiled=True)]
    all_to_all x1, blocking collectives: 128 us -> 103 us  [local(): lax.all_to_all(projector_weight, MP, split_axis=1, concat_axis=0, tiled=T...]
    unnamed x5 -> x8, local copies, waits for them, and re-layouts: 7.75 us -> 19.7 us
  transfers between devices with their start and end apart: 2 -> 1, of which waited for: 2 -> 1; matrix products, arithmetic and copies ran while one was open for 4% -> 2% of each run, Pallas kernels for 0% -> 0%
where the time goes in v1:
time: 656 us; the launch traced here: 655 us
  blocking collectives  462 us (70%)
  waiting for transfers between devices  89.2 us (14%)
  matrix products  39.5 us (6%)
  local copies, waits for them, and re-layouts  34.9 us (5%)
  between operations  19.8 us (3%)
  other arithmetic  9.4 us (1%)
    all_to_all x1, blocking collectives, local(): lax.all_to_all(jnp.stack([crop_hidden] * lax.axis_size(MP)), MP, 0, 0)  281 us
    all_to_all x1, blocking collectives, local(): lax.all_to_all(projector_weight, MP, split_axis=1, concat_axis=0, tiled=T...  103 us
    psum x1, waiting for transfers between devices, local(): lax.psum(partial_gram.astype(jnp.bfloat16), MP).astype(jnp.float32)  89.2 us
    all_to_all x1, blocking collectives, local(): lax.all_to_all(by_crop, DP, split_axis=1, concat_axis=2, tiled=True)  43.5 us
    psum x4, blocking collectives, by_axis(): return functools.reduce(lax.psum, axes, x)  34.8 us
    unnamed x8, local copies, waits for them, and re-layouts  19.7 us
    dot_general x1, matrix products, local(): lax.dot_general(column_block, flat_piece, (((0,), (1,)), ((), ())), prefe...  18.9 us
    dot_general x1, matrix products, local(): jnp.einsum('jcr,jcs->crs', centered, centered, precision=highest)  16.8 us
  transfers between devices with their start and end apart: 1, of which 1 were waited for; matrix products, arithmetic and copies ran while one was open for 2% of the time, Pallas kernels for 0%

profile of v1, /device:TPU:0, one launch (start us, length us, event | category | flops | bytes accessed | tf_op | source)
XLA Modules:
  0.0 655.4 jit_solution(5738952224861552890)
XLA Ops:
  7.2 0.0 all-reduce.6.cloned.1.call-start
  7.2 11.9 %copy.9 = bf16[512,8192]{0,1:T(8,128)(2,1)} copy(bf16[512,8192]{1,0:T(8,128)(2,1)} %param.4) | data formatting | bytes 16777216 | tf_op args[1]
  19.1 12.3 %copy.10 = bf16[512,16,512]{2,0,1:T(8,128)(2,1)} copy(bf16[512,16,512]{0,2,1:T(8,128)(2,1)} %bitcast.35) | data formatting | bytes 16777216 | tf_op jit(solution)/shard_map/all_to_all | solution.py:23
  31.4 0.0 copy-start.1
  31.4 103.2 %all_to_all.33 = bf16[512,16,512]{2,0,1:T(8,128)(2,1)} all-to-all(bf16[512,16,512]{2,0,1:T(8,128)(2,1)} %copy.10), channel_id=1, replica_groups=mesh['dp_0'=4,'dp_1'=2,'mp_0'=4,'mp_1'=4] {'mp_0','mp_1'}, dimensions={1} | all-to-all | bytes 16777216 | tf_op jit(solution)/shard_map/all_to_all | solution.py:23
  134.6 0.0 copy-done.1
  134.6 2.9 stack.12
  137.5 281.0 %all_to_all.34 = bf16[16,8,192,512]{3,2,1,0:T(8,128)(2,1)} all-to-all(bf16[16,8,192,512]{3,2,1,0:T(8,128)(2,1)S(1)} %stack.12), channel_id=1, replica_groups=mesh['dp_0'=4,'dp_1'=2,'mp_0'=4,'mp_1'=4] {'mp_0','mp_1'}, dimensions={0} | all-to-all | bytes 50331648 | tf_op jit(solution)/shard_map/all_to_all | solution.py:25
  418.5 18.9 %fusion.5 = f32[512,8,192]{0,2,1:T(8,128)S(1)} fusion(bf16[16,8,192,512]{3,2,1,0:T(8,128)(2,1)} %all_to_all.34, bf16[512,16,512]{2,0,1:T(8,128)(2,1)} %all_to_all.33), kind=kOutput, calls=%fused_computation.10 | convolution fusion | flops 12884901888 | bytes 36700160 | tf_op jit(solution)/shard_map/dot_general | solution.py:28
  437.4 0.0 copy-start
  437.4 1.7 copy-done
  439.1 43.5 %all_to_all.35 = f32[512,8,192]{0,2,1:T(8,128)S(1)} all-to-all(f32[512,8,192]{0,2,1:T(8,128)S(1)} %fusion.5), channel_id=1, replica_groups=mesh['dp_0'=4,'dp_1'=2,'mp_0'=4,'mp_1'=4] {'dp_0','dp_1'}, dimensions={1} | all-to-all | bytes 6291456 | tf_op jit(solution)/shard_map/all_to_all | solution.py:41
  482.6 0.3 reduce_sum.65
  482.9 0.6 multiply_reduce_fusion.1
  483.4 16.8 %fusion.4 = bf16[1,1536,1536]{2,1,0:T(8,128)(2,1)} fusion(f32[512,1536]{0,1:T(8,128)S(1)} %bitcast.36), kind=kOutput, calls=%fused_computation.6 | convolution fusion | flops 14497873920 | bytes 7864320 | tf_op jit(solution)/shard_map/jcr,jcs->crs/dot_general | solution.py:49
  500.2 0.0 copy-start.2
  500.2 0.0 all-reduce.6.cloned.1.call-update
  500.2 0.7 copy-done.2
  500.9 3.9 convolution_bitcast_fusion
  504.8 0.1 slice_bitcast_fusion.1
  504.9 2.0 multiply_reduce_fusion.2
  508.1 5.4 copy.12
  513.6 0.7 multiply_reduce_fusion.4
  514.2 89.2 %all-reduce.6.cloned.1.call-done = bf16[1,1536,1536]{2,1,0:T(8,128)(2,1)} async-done(((bf16[1,1536,1536]{2,1,0:T(8,128)(2,1)}), bf16[1,1536,1536]{2,1,0:T(8,128)(2,1)}) %all-reduce.6.cloned.1.call-update) | async-done | bytes 4718608 | tf_op jit(solution)/shard_map/psum | solution.py:50
  603.4 5.3 multiply_reduce_fusion
  610.0 11.3 %all-reduce.2 = (f32[]{:T(128)}, f32[]{:T(128)}, f32[]{:T(128)}) all-reduce(f32[]{:T(128)S(6)} %add.47, f32[]{:T(128)} %get-tuple-element.11, f32[]{:T(128)S(6)} %sub.61), channel_id=1, replica_groups=mesh['dp_0'=4,'dp_1'=2,'mp_0'=4,'mp_1'=4] {'dp_0'}, use_global_device_ids=true, to_apply=%region_2.0 | all-reduce | flops 3 | bytes 24 | tf_op jit(solution)/shard_map/psum | solution.py:16
  621.2 3.2 all-reduce.3
  624.4 11.0 %all-reduce.1 = (f32[]{:T(128)}, f32[]{:T(128)}, f32[]{:T(128)}) all-reduce(f32[]{:T(128)} %get-tuple-element.21, f32[]{:T(128)} %get-tuple-element.22, f32[]{:T(128)} %get-tuple-element.23), channel_id=1, replica_groups=mesh['dp_0'=4,'dp_1'=2,'mp_0'=4,'mp_1'=4] {'mp_0'}, use_global_device_ids=true, to_apply=%region_4.5 | all-reduce | flops 3 | bytes 24 | tf_op jit(solution)/shard_map/psum | solution.py:16
  635.3 9.4 %all-reduce = (f32[]{:T(128)}, f32[]{:T(128)}, f32[]{:T(128)}) all-reduce(f32[]{:T(128)} %get-tuple-element.15, f32[]{:T(128)} %get-tuple-element.16, f32[]{:T(128)} %get-tuple-element.17), channel_id=1, replica_groups=mesh['dp_0'=4,'dp_1'=2,'mp_0'=4,'mp_1'=4] {'mp_1'}, use_global_device_ids=true, to_apply=%region_5.6 | all-reduce | flops 3 | bytes 24 | tf_op jit(solution)/shard_map/psum | solution.py:16
  647.9 0.6 pad_maximum_fusion
  (1 shorter events, 0.0 us)
Async XLA Ops:
  7.2 596.2 %all-reduce.6.cloned.1.call-start = ((), (), s32[]{:S(2)}) async-start(), calls=%async_computation.3 | async-start | bytes 9437184 | tf_op jit(solution)/shard_map/psum | solution.py:50
  31.4 103.2 %copy-start.1 = (bf16[8,192,512]{2,1,0:T(8,128)(2,1)S(1)}, bf16[8,192,512]{2,1,0:T(8,128)(2,1)}, u32[]{:S(2)}) copy-start(bf16[8,192,512]{2,1,0:T(8,128)(2,1)} %param.3) | copy-start | bytes 4718596
  437.4 1.7 copy-start
  500.2 0.7 copy-start.2
Sparse Core Ops, SparseCore 0:
  500.3 103.0 all-reduce.5
